TPU v7x, 32 devices: a 4x4x1 block of a 4x4x8 slice. The times are simulated.
32 devices in a mesh: data: 1 (over z), outer: 4 (over y), expert: 8 (over x, core).
Axes of the slice: x: 4, y: 4, z: 1, core: 2. Of those that a mesh axis runs over, the one named last changes fastest.
The devices are a block of a 4x4x8 slice.
Arguments:
- x_disp: bfloat16 [32, 128, 8, 2048], P('data', ('outer', 'expert'))
- w_gate: bfloat16 [128, 2048, 768], P(('outer', 'expert'))
- w_up: bfloat16 [128, 2048, 768], P(('outer', 'expert'))
- w_down: bfloat16 [128, 768, 2048], P(('outer', 'expert'))
- slot_idx: int32 [4096, 8], P(('data', 'outer', 'expert'))
- expert_ids: int32 [4096, 8], P(('data', 'outer', 'expert'))
- gate_wts: float32 [4096, 8], P(('data', 'outer', 'expert'))
Outputs:
- output: bfloat16 [4096, 2048], P(('data', 'outer', 'expert'))
All inputs are finite; a program needn't handle non-finite values.
Results may differ from a plain program's by a relative error of at most 0.00826245.
Values are sent between devices in bfloat16 or wider.
A program may use at most 768 MiB of HBM per device.

v0:
```python
import jax
import jax.numpy as jnp
from jax import lax
from jax.sharding import PartitionSpec as P


def expert_rows(x_disp, w_gate, w_up, w_down):
    gate_proj = jnp.einsum("secd,edf->secf", x_disp, w_gate, preferred_element_type=jnp.float32)
    up_proj = jnp.einsum("secd,edf->secf", x_disp, w_up, preferred_element_type=jnp.float32)
    hidden = (jax.nn.silu(gate_proj) * up_proj).astype(jnp.bfloat16)
    return jnp.einsum("secf,efd->secd", hidden, w_down, preferred_element_type=jnp.float32).astype(jnp.bfloat16)


def weighted_sum(y_flat, capacity, slot_idx, expert_ids, gate_wts):
    kept_mask = slot_idx >= 0
    flat_idx = jnp.where(kept_mask, expert_ids * capacity + slot_idx, 0)
    weight = jnp.where(kept_mask, gate_wts, 0.0)
    picked = jnp.take(y_flat, flat_idx, axis=0)
    return jnp.sum(picked.astype(jnp.float32) * weight[:, :, None], axis=1).astype(jnp.bfloat16)


def solution(mesh):
    outer_devs = mesh.shape["outer"]
    inner_devs = mesh.shape["expert"]

    def local_step(x_disp, w_gate, w_up, w_down, slot_idx, expert_ids, gate_wts):
        group_devs, local_experts, capacity, model_width = x_disp.shape
        y_local = expert_rows(x_disp, w_gate, w_up, w_down)
        y_split = y_local.reshape(outer_devs, inner_devs, local_experts, capacity, model_width)
        y_inner = lax.all_to_all(y_split, "expert", 1, 1, tiled=True)
        y_recv = lax.all_to_all(y_inner, "outer", 0, 0, tiled=True)
        y_flat = y_recv.reshape(group_devs * local_experts * capacity, model_width)
        return weighted_sum(y_flat, capacity, slot_idx, expert_ids, gate_wts)

    expert_spec = P(("outer", "expert"))
    token_spec = P(("data", "outer", "expert"))
    return jax.shard_map(local_step, mesh=mesh, in_specs=(P("data", ("outer", "expert")), expert_spec, expert_spec, expert_spec, token_spec, token_spec, token_spec), out_specs=token_spec, check_vma=False)
```

profile of v0, /device:TPU:96, one launch (start us, length us, event | category | flops | bytes accessed | tf_op | source)
XLA Modules:
  0.0 163.6 jit_solution(2235222820454967290)
XLA Ops:
  0.0 12.5 %fusion.2 = f32[4,768,32,8]{1,2,3,0:T(8,128)} fusion(bf16[4,2048,768]{2,1,0:T(8,128)(2,1)} %param.9, bf16[32,4,8,2048]{3,2,1,0:T(8,128)(2,1)} %param.7), kind=kOutput, calls=%fused_computation.3 | convolution fusion | flops 3221225472 | bytes 19922944 | tf_op jit(solution)/shard_map/secd,edf->secf/dot_general | solution.py:9
  12.5 0.0 copy-start.3
  12.5 11.6 %fusion.11 = bf16[32,4,8,768]{3,0,2,1:T(8,128)(2,1)} fusion(f32[4,768,32,8]{1,2,3,0:T(8,128)} %fusion.2, bf16[32,4,8,2048]{3,2,1,0:T(8,128)(2,1)} %param.7, bf16[4,2048,768]{2,1,0:T(8,128)(2,1)} %param.8), kind=kOutput, calls=%fused_computation.13 | convolution fusion | flops 3225944064 | bytes 21495808 | tf_op jit(solution)/shard_map/secd,edf->secf/dot_general | solution.py:8
  24.0 0.0 copy-done.3
  24.0 5.9 %fusion.6 = bf16[4,32,8,2048]{3,2,1,0:T(8,128)(2,1)S(1)} fusion(bf16[4,768,2048]{2,1,0:T(8,128)(2,1)S(1)} %copy-done.3, bf16[32,4,8,768]{3,0,2,1:T(8,128)(2,1)} %fusion.11), kind=kOutput, calls=%fused_computation.9 | convolution fusion | flops 3223322624 | bytes 18350080 | tf_op jit(solution)/shard_map/secf,efd->secd/dot_general | solution.py:11
  29.9 0.3 copy.23
  30.2 53.6 %all_to_all.10 = bf16[4,8,4,8,2048]{4,3,0,2,1:T(8,128)(2,1)S(1)} all-to-all(bf16[4,8,4,8,2048]{4,3,0,2,1:T(8,128)(2,1)S(1)} %copy.23), channel_id=1, replica_groups=mesh['data'=1,'outer'=4,'expert'=8] {'expert'}, dimensions={1} | all-to-all | bytes 8388608 | tf_op jit(solution)/shard_map/all_to_all | solution.py:30
  83.8 2.3 %copy.24 = bf16[4,8,4,8,2048]{4,3,1,2,0:T(8,128)(2,1)} copy(bf16[4,8,4,8,2048]{4,3,0,2,1:T(8,128)(2,1)S(1)} %all_to_all.10) | data formatting | bytes 8388608 | tf_op jit(solution)/shard_map/all_to_all | solution.py:30
  86.1 0.0 copy-start
  86.1 0.0 copy-start.2
  86.1 0.0 copy-start.1
  86.1 6.1 %all-to-all-start.1 = ((bf16[4,8,4,8,2048]{4,3,1,2,0:T(8,128)(2,1)}), bf16[4,8,4,8,2048]{4,3,1,2,0:T(8,128)(2,1)}, u32[]{:S(2)}, u32[]{:S(2)}) async-start(bf16[4,8,4,8,2048]{4,3,1,2,0:T(8,128)(2,1)} %copy.24), calls=%async_computation.1 | async-start | bytes 8388608 | tf_op jit(solution)/shard_map/all_to_all | solution.py:31
  92.1 0.0 copy-done
  92.1 0.0 copy-done.2
  92.2 0.1 copy.26
  92.3 0.1 reshape.16
  92.3 0.0 copy-done.1
  92.4 0.1 copy.27
  92.5 0.1 copy.19
  92.6 48.4 %all-to-all-done.1 = bf16[4,8,4,8,2048]{4,3,1,2,0:T(8,128)(2,1)} async-done(((bf16[4,8,4,8,2048]{4,3,1,2,0:T(8,128)(2,1)}), bf16[4,8,4,8,2048]{4,3,1,2,0:T(8,128)(2,1)}, u32[]{:S(2)}, u32[]{:S(2)}) %all-to-all-start.1) | async-done | bytes 4194336 | tf_op jit(solution)/shard_map/all_to_all | solution.py:31
  141.0 4.7 %copy.25 = bf16[4,8,4,8,2048]{4,3,2,1,0:T(8,128)(2,1)} copy(bf16[4,8,4,8,2048]{4,3,1,2,0:T(8,128)(2,1)} %all-to-all-done.1) | data formatting | bytes 8388608 | tf_op jit(solution)/shard_map/all_to_all | solution.py:31
  145.8 11.5 %gather_fusion = bf16[1024,2048]{1,0:T(8,128)(2,1)} fusion(bf16[1024,2048]{1,0:T(8,128)(2,1)} %bitcast.44, s32[1024]{0:T(1024)S(1)} %broadcast_clamp_fusion), kind=kCustom, calls=%fused_computation | custom fusion | bytes 8392704 | tf_op jit(solution)/shard_map/jit(_take)/gather | solution.py:18
  157.3 6.3 %multiply_reduce_fusion = bf16[128,2048]{1,0:T(8,128)(2,1)} fusion(bf16[1024,2048]{1,0:T(8,128)(2,1)} %gather_fusion, f32[128,8]{1,0:T(8,128)S(1)} %copy.27, pred[128,8]{1,0:T(8,128)(4,1)S(1)} %copy.19), kind=kLoop, calls=%fused_computation.7 | loop fusion | flops 8126464 | bytes 4723712 | tf_op jit(solution)/shard_map/reduce_sum | solution.py:19
  (3 shorter events, 0.0 us)
Async XLA Ops:
  12.5 11.6 %copy-start.3 = (bf16[4,768,2048]{2,1,0:T(8,128)(2,1)S(1)}, bf16[4,768,2048]{2,1,0:T(8,128)(2,1)}, u32[]{:S(2)}) copy-start(bf16[4,768,2048]{2,1,0:T(8,128)(2,1)} %param.10) | copy-start | bytes 37748740
  86.1 6.1 %copy-start = (s32[128,8]{0,1:T(8,128)S(1)}, s32[128,8]{0,1:T(8,128)}, u32[]{:S(2)}) copy-start(s32[128,8]{0,1:T(8,128)} %param.11) | copy-start | bytes 12292
  86.1 6.1 %copy-start.2 = (s32[128,8]{0,1:T(8,128)S(1)}, s32[128,8]{0,1:T(8,128)}, u32[]{:S(2)}) copy-start(s32[128,8]{0,1:T(8,128)} %param.12) | copy-start | bytes 12292
  86.1 6.3 %copy-start.1 = (f32[128,8]{0,1:T(8,128)S(1)}, f32[128,8]{0,1:T(8,128)}, u32[]{:S(2)}) copy-start(f32[128,8]{0,1:T(8,128)} %param.13) | copy-start | bytes 12292
  86.1 55.0 %all-to-all-start.1 = ((bf16[4,8,4,8,2048]{4,3,1,2,0:T(8,128)(2,1)}), bf16[4,8,4,8,2048]{4,3,1,2,0:T(8,128)(2,1)}, u32[]{:S(2)}, u32[]{:S(2)}) async-start(bf16[4,8,4,8,2048]{4,3,1,2,0:T(8,128)(2,1)} %copy.24), calls=%async_computation.1 | async-start | bytes 8388608 | tf_op jit(solution)/shard_map/all_to_all | solution.py:31
where the time goes:
time: 164 us
  blocking collectives  53.6 us (33%)
  waiting for transfers between devices  48.4 us (30%)
  matrix products  29.9 us (18%)
  local copies, waits for them, and re-layouts  19.3 us (12%)
  other arithmetic  6.29 us (4%)
  starting transfers between devices  6.06 us (4%)
    all_to_all x1, blocking collectives, local_step(): y_inner = lax.all_to_all(y_split, 'expert', 1, 1, tiled=True)  53.6 us
    all_to_all x1, waiting for transfers between devices, local_step(): y_recv = lax.all_to_all(y_inner, 'outer', 0, 0, tiled=True)  48.4 us
    dot_general x1, matrix products, expert_rows(): jnp.einsum('secd,edf->secf', x_disp, w_up, preferred_element_type=jnp.flo...  12.5 us
    dot_general x1, matrix products, expert_rows(): jnp.einsum('secd,edf->secf', x_disp, w_gate, preferred_element_type=jnp.f...  11.6 us
    gather x1, local copies, waits for them, and re-layouts, weighted_sum(): picked = jnp.take(y_flat, flat_idx, axis=0)  11.5 us
    reduce_sum x1, other arithmetic, weighted_sum(): jnp.sum(picked.astype(jnp.float32) * weight[:, :, None], axis=1)  6.27 us
    all_to_all x1, starting transfers between devices, local_step(): y_recv = lax.all_to_all(y_inner, 'outer', 0, 0, tiled=True)  6.06 us
    dot_general x1, matrix products, expert_rows(): jnp.einsum('secf,efd->secd', hidden, w_down, preferred_element_type=jnp.f...  5.87 us
  transfers between devices with their start and end apart: 1, of which 1 were waited for; matrix products, arithmetic and copies ran while one was open for 0% of the time, Pallas kernels for 0%

commit v1 on v0

v1 whole, which is shorter than its diff:
```python
import jax
import jax.numpy as jnp
from jax import lax
from jax.experimental import pallas as pl
from jax.experimental.pallas import tpu as pltpu
from jax.sharding import PartitionSpec as P

MESH_ID = pl.DeviceIdType.MESH
FF_CHUNK = 256
D_CHUNK = 512
BF16_MAX = 3.3895313892515355e38


def ring_distance(step, size):
    return min(step, size - step)


def peer_offsets(outer_devs, inner_devs):
    chips = inner_devs // 2
    steps = [(dy, dx, flip) for dx in range(chips) for dy in range(outer_devs) for flip in range(2)]
    steps = [s for s in steps if s != (0, 0, 0)]
    return sorted(steps, key=lambda s: -(ring_distance(s[0], outer_devs) + ring_distance(s[1], chips)))


def make_kernel(outer_devs, inner_devs, experts, capacity, width, ff, tokens, top):
    group = outer_devs * inner_devs
    rows = group * capacity
    chips = inner_devs // 2
    offsets = peer_offsets(outer_devs, inner_devs)
    n_ff, n_d = ff // FF_CHUNK, width // D_CHUNK

    def kernel(x_hbm, wg_hbm, wu_hbm, wd_hbm, slot_ref, eid_ref, gate_ref, out_ref,
               x_buf, wg_buf, wu_buf, wd_buf, h_buf, send_buf, recv_buf, acc, w_buf, used_buf,
               x_sem, g_sem, u_sem, d_sem, send_sem, recv_sem):
        row = lax.axis_index("outer")
        col = lax.axis_index("expert")
        me = row * inner_devs + col
        chip, core = col // 2, lax.rem(col, 2)

        def peer(offset):
            dy, dx, flip = offset
            return lax.rem(row + dy, outer_devs), lax.rem(chip + dx, chips) * 2 + lax.rem(core + flip, 2)

        def x_copy(e):
            return pltpu.make_async_copy(x_hbm.at[:, e], x_buf.at[e], x_sem.at[e])

        def gate_copy(e, f):
            cols = pl.ds(f * FF_CHUNK, FF_CHUNK)
            return pltpu.make_async_copy(wg_hbm.at[e, :, cols], wg_buf.at[e, :, cols], g_sem.at[e, f])

        def up_copy(e, f):
            cols = pl.ds(f * FF_CHUNK, FF_CHUNK)
            return pltpu.make_async_copy(wu_hbm.at[e, :, cols], wu_buf.at[e, :, cols], u_sem.at[e, f])

        def down_copy(e, d):
            cols = pl.ds(d * D_CHUNK, D_CHUNK)
            return pltpu.make_async_copy(wd_hbm.at[e, :, cols], wd_buf.at[e, :, cols], d_sem.at[e, d])

        def remote(e, offset):
            py, px = peer(offset)
            return pltpu.make_async_remote_copy(
                src_ref=send_buf.at[e, py * inner_devs + px], dst_ref=recv_buf.at[e, me],
                send_sem=send_sem.at[e], recv_sem=recv_sem.at[e],
                device_id={"outer": py, "expert": px}, device_id_type=MESH_ID)

        for e in range(experts):
            x_copy(e).start()
            for f in range(n_ff):
                gate_copy(e, f).start()
                up_copy(e, f).start()
            for d in range(n_d):
                down_copy(e, d).start()

        barrier = pltpu.get_barrier_semaphore()
        for offset in offsets:
            py, px = peer(offset)
            pl.semaphore_signal(barrier, inc=1, device_id={"outer": py, "expert": px}, device_id_type=MESH_ID)

        def expert_step(e):
            x_copy(e).wait()
            x_rows = x_buf[e].reshape(rows, width)
            for f in range(n_ff):
                cols = pl.ds(f * FF_CHUNK, FF_CHUNK)
                gate_copy(e, f).wait()
                gate_proj = jnp.dot(x_rows, wg_buf[e, :, cols], preferred_element_type=jnp.float32)
                up_copy(e, f).wait()
                up_proj = jnp.dot(x_rows, wu_buf[e, :, cols], preferred_element_type=jnp.float32)
                h_buf[:, cols] = (jax.nn.silu(gate_proj) * up_proj).astype(jnp.bfloat16)
            hidden = h_buf[...]
            for d in range(n_d):
                cols = pl.ds(d * D_CHUNK, D_CHUNK)
                down_copy(e, d).wait()
                y = jnp.dot(hidden, wd_buf[e, :, cols], preferred_element_type=jnp.float32)
                send_buf[e, :, :, cols] = y.reshape(group, capacity, D_CHUNK).astype(jnp.bfloat16)

        def send_step(e):
            for offset in offsets:
                remote(e, offset).start()
            recv_buf[e, me] = send_buf[e, me]

        expert_step(0)
        pl.semaphore_wait(barrier, group - 1)
        send_step(0)

        @pl.loop(1, experts)
        def _(e):
            expert_step(e)
            send_step(e)

        slots = slot_ref[...]
        keys = jnp.where(slots >= 0, eid_ref[...] * capacity + slots, -1)
        gates = gate_ref[...]
        line = lax.broadcasted_iota(jnp.int32, (rows, tokens), 0)
        for e in range(experts):
            row_key = (line // capacity) * (experts * capacity) + e * capacity + lax.rem(line, capacity)
            weight = jnp.zeros((rows, tokens), jnp.float32)
            for j in range(top):
                weight = weight + jnp.where(row_key == keys[j:j + 1], gates[j:j + 1], 0.0)
            used_buf[e] = jnp.broadcast_to(jnp.max(weight, axis=1, keepdims=True), (rows, 128))
            weight = weight.T
            high = jnp.minimum(weight, BF16_MAX).astype(jnp.bfloat16)
            rest = weight - high.astype(jnp.float32)
            mid = rest.astype(jnp.bfloat16)
            low = (rest - mid.astype(jnp.float32)).astype(jnp.bfloat16)
            w_buf[e, 0:tokens] = high
            w_buf[e, tokens:2 * tokens] = mid
            w_buf[e, 2 * tokens:3 * tokens] = low

        for e in range(experts):
            pltpu.make_async_remote_copy(
                src_ref=send_buf.at[e, pl.ds(0, group - 1)], dst_ref=recv_buf.at[e, pl.ds(0, group - 1)],
                send_sem=send_sem.at[e], recv_sem=recv_sem.at[e],
                device_id={"outer": row, "expert": col}, device_id_type=MESH_ID).wait_recv()
            used = used_buf[e] > 0.0
            for d in range(n_d):
                cols = pl.ds(d * D_CHUNK, D_CHUNK)
                y = recv_buf[e, :, :, cols].astype(jnp.float32).reshape(rows, D_CHUNK)
                y = jnp.where(jnp.concatenate([used] * (D_CHUNK // 128), axis=1), y, 0.0).astype(jnp.bfloat16)
                part = jnp.dot(w_buf[e], y, preferred_element_type=jnp.float32)
                total = part[0:tokens] + (part[tokens:2 * tokens] + part[2 * tokens:3 * tokens])
                if e > 0:
                    total = acc[:, cols] + total
                if e < experts - 1:
                    acc[:, cols] = total
                else:
                    out_ref[:, cols] = total.astype(jnp.bfloat16)

        for e in range(experts):
            pltpu.make_async_remote_copy(
                src_ref=send_buf.at[e, pl.ds(0, group - 1)], dst_ref=recv_buf.at[e, pl.ds(0, group - 1)],
                send_sem=send_sem.at[e], recv_sem=recv_sem.at[e],
                device_id={"outer": row, "expert": col}, device_id_type=MESH_ID).wait_send()

    return kernel


def solution(mesh):
    outer_devs = mesh.shape["outer"]
    inner_devs = mesh.shape["expert"]

    def local_step(x_disp, w_gate, w_up, w_down, slot_idx, expert_ids, gate_wts):
        group, experts, capacity, width = x_disp.shape
        ff = w_gate.shape[2]
        tokens, top = slot_idx.shape
        rows = group * capacity
        n_ff, n_d = ff // FF_CHUNK, width // D_CHUNK
        bf16, f32 = jnp.bfloat16, jnp.float32
        hbm = pl.BlockSpec(memory_space=pl.ANY)
        vmem = pl.BlockSpec(memory_space=pltpu.VMEM)
        return pl.pallas_call(
            make_kernel(outer_devs, inner_devs, experts, capacity, width, ff, tokens, top),
            out_shape=jax.ShapeDtypeStruct((tokens, width), bf16),
            in_specs=[hbm] * 4 + [vmem] * 3,
            out_specs=vmem,
            scratch_shapes=[
                pltpu.VMEM((experts, group, capacity, width), bf16),
                pltpu.VMEM((experts, width, ff), bf16),
                pltpu.VMEM((experts, width, ff), bf16),
                pltpu.VMEM((experts, ff, width), bf16),
                pltpu.VMEM((rows, ff), bf16),
                pltpu.VMEM((experts, group, capacity, width), bf16),
                pltpu.VMEM((experts, group, capacity, width), bf16),
                pltpu.VMEM((tokens, width), f32),
                pltpu.VMEM((experts, 3 * tokens, rows), bf16),
                pltpu.VMEM((experts, rows, 128), f32),
                pltpu.SemaphoreType.DMA((experts,)),
                pltpu.SemaphoreType.DMA((experts, n_ff)),
                pltpu.SemaphoreType.DMA((experts, n_ff)),
                pltpu.SemaphoreType.DMA((experts, n_d)),
                pltpu.SemaphoreType.DMA((experts,)),
                pltpu.SemaphoreType.DMA((experts,)),
            ],
            compiler_params=pltpu.CompilerParams(collective_id=0, has_side_effects=True, vmem_limit_bytes=67043328),
        )(x_disp, w_gate, w_up, w_down, slot_idx.T, expert_ids.T, gate_wts.T)

    expert_spec = P(("outer", "expert"))
    token_spec = P(("data", "outer", "expert"))
    return jax.shard_map(local_step, mesh=mesh, in_specs=(P("data", ("outer", "expert")), expert_spec, expert_spec, expert_spec, token_spec, token_spec, token_spec), out_specs=token_spec, check_vma=False)
```

time: 164 us -> 73 us (0.45)
  the two profiles are of different devices: /device:TPU:96 before, /device:TPU:101 now
where the time goes in v1:
time: 73 us; the launch traced here: 72.9 us
  Pallas kernels  71 us (97%)
  local copies, waits for them, and re-layouts  1.88 us (3%)
    pallas_call x1, Pallas kernels, local_step(): pl.pallas_call(make_kernel(outer_devs, inner_devs, experts, capacity, wid...  71 us
    unnamed x1, local copies, waits for them, and re-layouts  1.88 us

profile of v1, /device:TPU:101, one launch (start us, length us, event | category | flops | bytes accessed | tf_op | source)
XLA Modules:
  0.0 72.9 jit_solution(16350958557954994268)
XLA Ops:
  0.0 71.0 %shard_map.73 = bf16[128,2048]{1,0:T(8,128)(2,1)} custom-call(bf16[32,4,8,2048]{3,2,1,0:T(8,128)(2,1)} %x_hbm.1, bf16[4,2048,768]{2,1,0:T(8,128)(2,1)} %wg_hbm.1, bf16[4,2048,768]{2,1,0:T(8,128)(2,1)} %wu_hbm.1, bf16[4,768,2048]{2,1,0:T(8,128)(2,1)} %wd_hbm.1, s32[8,128]{1,0:T(8,128)} %bitcast.3, s32[8,128]{1,0:T(8,128)} %bitcast.4, f32[8,128]{1,0:T(8,128)} %bitcast.5), custom_call_target="tpu_custom_call" | custom-call | tf_op jit(solution)/shard_map/pallas_call | solution.py:170
  71.0 1.9 %copy.9 = bf16[128,2048]{1,0:T(8,128)(2,1)} copy(bf16[128,2048]{1,0:T(8,128)(2,1)} %shard_map.73) | data formatting | bytes 1048576

commit v2 on v0

v2 whole, which is shorter than its diff:
```python
import jax
import jax.numpy as jnp
from jax import lax
from jax.experimental import pallas as pl
from jax.experimental.pallas import tpu as pltpu
from jax.sharding import PartitionSpec as P

MESH_ID = pl.DeviceIdType.MESH
CORES = 2
HALVES = 2
QUARTERS = 2
K_PARTS = 2
WEIGHT_SLOTS = 3
VMEM_LIMIT = 67043328
BF16_MAX = 3.3895313892515355e38


def make_kernel(ring, experts, capacity, width, ff, tokens, top):
    peers = ring * CORES
    group = ring * peers
    rows = group * capacity
    part_rows = experts * peers * capacity
    half = width // HALVES
    quarter = half // QUARTERS
    k_size = width // K_PARTS
    mid = tokens // 2

    def kernel(x_hbm, wg_hbm, wu_hbm, wd_hbm, slot_hbm, eid_hbm, gate_hbm, out_ref,
               x_buf, wg_buf, wu_buf, wd_buf, slot_buf, eid_buf, gate_buf, send_buf, recv_buf,
               routes, w_buf, used_buf, far_out, far_in, near_out, near_in, acc,
               x_sem, g_sem, u_sem, d_sem, route_sem, p1_send, p1_recv, rt_send, rt_recv,
               far_send, far_recv, own_send, own_recv, sum_send, sum_recv):
        row = lax.axis_index("outer")
        col = lax.axis_index("expert")
        chip, core = col // CORES, lax.rem(col, CORES)
        place = (row, chip)
        source = (col, row * CORES + core)

        def shift(start, step):
            return lax.rem(start + step, ring)

        def ring_peer(h, step):
            if h == 0:
                return {"outer": shift(row, step), "expert": col}
            return {"outer": row, "expert": shift(chip, step) * CORES + core}

        def first_peer(h, step, flip):
            other = lax.rem(core + flip, CORES)
            if h == 0:
                to = shift(chip, step)
                return {"outer": row, "expert": to * CORES + other}, to, other
            to = shift(row, step)
            return {"outer": to, "expert": chip * CORES + other}, to, other

        def rows_for(h, e, to, other, cols):
            if h == 0:
                return send_buf.at[e, :, to, other, :, cols]
            return send_buf.at[e, to, :, other, :, cols]

        hops = [(2, 0), (2, 1), (1, 0), (ring - 1, 0), (1, 1), (ring - 1, 1), (0, 1)]

        def first_copy(h, e, q, step, flip):
            peer, to, other = first_peer(h, step, flip)
            return pltpu.make_async_remote_copy(
                src_ref=rows_for(h, e, to, other, pl.ds(h * half + q * quarter, quarter)),
                dst_ref=recv_buf.at[h, e, source[h], :, :, pl.ds(q * quarter, quarter)],
                send_sem=p1_send.at[h, e, q], recv_sem=p1_recv.at[h, e, q],
                device_id=peer, device_id_type=MESH_ID)

        def first_all(h, e, q):
            ref = recv_buf.at[h, e, pl.ds(0, peers - 1), :, :, pl.ds(q * quarter, quarter)]
            return pltpu.make_async_remote_copy(
                src_ref=ref, dst_ref=ref, send_sem=p1_send.at[h, e, q], recv_sem=p1_recv.at[h, e, q],
                device_id=ring_peer(h, 1), device_id_type=MESH_ID)

        def route_copy(h, step):
            return pltpu.make_async_remote_copy(
                src_ref=routes.at[h, 0], dst_ref=routes.at[h, ring - step],
                send_sem=rt_send.at[0], recv_sem=rt_recv.at[0],
                device_id=ring_peer(h, step), device_id_type=MESH_ID)

        def route_all():
            ref = routes.at[:, pl.ds(1, ring - 1)]
            return pltpu.make_async_remote_copy(
                src_ref=ref, dst_ref=ref, send_sem=rt_send.at[0], recv_sem=rt_recv.at[0],
                device_id=ring_peer(0, 1), device_id_type=MESH_ID)

        def near_step(way):
            return 1 if way == 0 else ring - 1

        def relay_part(way):
            return pl.ds(way * mid, mid)

        def own_part(way):
            return pl.ds((1 - way) * mid, mid)

        def far_copy(h, q, way):
            return pltpu.make_async_remote_copy(
                src_ref=far_out.at[h, q, way], dst_ref=far_in.at[h, q, way],
                send_sem=far_send.at[h, q, way], recv_sem=far_recv.at[h, q, way],
                device_id=ring_peer(h, near_step(way)), device_id_type=MESH_ID)

        def own_copy(h, q, way):
            return pltpu.make_async_remote_copy(
                src_ref=near_out.at[h, q, way, own_part(way)], dst_ref=near_in.at[h, q, way, own_part(way)],
                send_sem=own_send.at[h, q, way], recv_sem=own_recv.at[h, q, way],
                device_id=ring_peer(h, near_step(way)), device_id_type=MESH_ID)

        def sum_copy(h, q, way):
            return pltpu.make_async_remote_copy(
                src_ref=near_out.at[h, q, way, relay_part(way)], dst_ref=near_in.at[h, q, way, relay_part(way)],
                send_sem=sum_send.at[h, q, way], recv_sem=sum_recv.at[h, q, way],
                device_id=ring_peer(h, near_step(way)), device_id_type=MESH_ID)

        def part_copies(k):
            cols = pl.ds(k * k_size, k_size)
            return (pltpu.make_async_copy(x_hbm.at[:, 0, :, cols], x_buf.at[0, :, :, cols], x_sem.at[k]),
                    pltpu.make_async_copy(wg_hbm.at[0, cols], wg_buf.at[0, cols], g_sem.at[k]),
                    pltpu.make_async_copy(wu_hbm.at[0, cols], wu_buf.at[0, cols], u_sem.at[k]))

        def down_part_copy(h):
            cols = pl.ds(h * half, half)
            return pltpu.make_async_copy(wd_hbm.at[0, :, cols], wd_buf.at[0, :, cols], d_sem.at[h])

        def weight_copies(e):
            slot = lax.rem(e, WEIGHT_SLOTS)
            return (pltpu.make_async_copy(x_hbm.at[:, e], x_buf.at[slot], x_sem.at[K_PARTS + e]),
                    pltpu.make_async_copy(wg_hbm.at[e], wg_buf.at[slot], g_sem.at[K_PARTS + e]),
                    pltpu.make_async_copy(wu_hbm.at[e], wu_buf.at[slot], u_sem.at[K_PARTS + e]),
                    pltpu.make_async_copy(wd_hbm.at[e], wd_buf.at[slot], d_sem.at[HALVES + e]))

        def token_copies():
            return (pltpu.make_async_copy(slot_hbm, slot_buf, route_sem.at[0]),
                    pltpu.make_async_copy(eid_hbm, eid_buf, route_sem.at[1]),
                    pltpu.make_async_copy(gate_hbm, gate_buf, route_sem.at[2]))

        for k in range(K_PARTS):
            for copy in part_copies(k):
                copy.start()
        greet = [first_peer(h, step, flip)[0] for h in range(HALVES) for step, flip in hops[:-1]] + [first_peer(0, 0, 1)[0]]
        barrier = pltpu.get_barrier_semaphore()
        for peer in greet:
            pl.semaphore_signal(barrier, inc=1, device_id=peer, device_id_type=MESH_ID)
        for h in range(HALVES):
            down_part_copy(h).start()
        for copy in token_copies():
            copy.start()
        for e in range(1, WEIGHT_SLOTS):
            for copy in weight_copies(e):
                copy.start()

        def first_send(h, e):
            for q in range(QUARTERS):
                for step, flip in hops:
                    first_copy(h, e, q, step, flip).start()
            cols = pl.ds(h * half, half)
            if h == 0:
                recv_buf[h, e, source[h]] = send_buf[e, :, chip, core, :, cols]
            else:
                recv_buf[h, e, source[h]] = send_buf[e, row, :, core, :, cols]

        def activation(gate_proj, up_proj):
            return (jax.nn.silu(gate_proj) * up_proj).astype(jnp.bfloat16)

        def down_step(e, slot, h, hidden):
            cols = pl.ds(h * half, half)
            y = jnp.dot(hidden, wd_buf[slot, :, cols], preferred_element_type=jnp.float32)
            send_buf[e, :, :, :, :, cols] = y.reshape(ring, ring, CORES, capacity, half).astype(jnp.bfloat16)

        gate_proj = up_proj = None
        for k in range(K_PARTS):
            for copy in part_copies(k):
                copy.wait()
            cols = pl.ds(k * k_size, k_size)
            x_rows = x_buf[0, :, :, cols].reshape(rows, k_size)
            gate_part = jnp.dot(x_rows, wg_buf[0, cols], preferred_element_type=jnp.float32)
            up_part = jnp.dot(x_rows, wu_buf[0, cols], preferred_element_type=jnp.float32)
            gate_proj = gate_part if gate_proj is None else gate_proj + gate_part
            up_proj = up_part if up_proj is None else up_proj + up_part
        hidden = activation(gate_proj, up_proj)
        for h in range(HALVES):
            down_part_copy(h).wait()
            down_step(0, 0, h, hidden)
            if h == 0:
                pl.semaphore_wait(barrier, len(greet))
            first_send(h, 0)
        for e in range(WEIGHT_SLOTS, experts):
            for copy in weight_copies(e):
                copy.start()

        for copy in token_copies():
            copy.wait()
        slots = slot_buf[...]
        keys = jnp.where(slots >= 0, eid_buf[...] * capacity + slots, -1).astype(jnp.float32)
        for h in range(HALVES):
            routes[h, 0, 0:top] = keys
            routes[h, 0, top:2 * top] = gate_buf[...]
        for h in range(HALVES):
            for step in range(1, ring):
                route_copy(h, step).start()

        @pl.loop(1, experts)
        def _(e):
            slot = lax.rem(e, WEIGHT_SLOTS)
            x_copy, gate_copy, up_copy, down_copy = weight_copies(e)
            x_copy.wait()
            x_rows = x_buf[slot].reshape(rows, width)
            gate_copy.wait()
            gate_proj = jnp.dot(x_rows, wg_buf[slot], preferred_element_type=jnp.float32)
            up_copy.wait()
            up_proj = jnp.dot(x_rows, wu_buf[slot], preferred_element_type=jnp.float32)
            hidden = activation(gate_proj, up_proj)
            down_copy.wait()
            for h in range(HALVES):
                down_step(e, slot, h, hidden)
                first_send(h, e)

        route_all().wait_recv()
        line = lax.broadcasted_iota(jnp.int32, (part_rows, tokens), 0)
        local = line // (peers * capacity)
        src = lax.rem(line // capacity, peers)
        device = (row * peers + src, (src // CORES) * peers + chip * CORES + lax.rem(src, CORES))
        for h in range(HALVES):
            row_key = ((device[h] * experts + local) * capacity + lax.rem(line, capacity)).astype(jnp.float32)
            for step in range(ring):
                weight = jnp.zeros((part_rows, tokens), jnp.float32)
                for j in range(top):
                    weight = weight + jnp.where(row_key == routes[h, step, j:j + 1], routes[h, step, top + j:top + j + 1], 0.0)
                used_buf[h, step] = jnp.broadcast_to(jnp.max(weight, axis=1, keepdims=True), (part_rows, 128))
                weight = weight.T
                high = jnp.minimum(weight, BF16_MAX).astype(jnp.bfloat16)
                rest = weight - high.astype(jnp.float32)
                middle = rest.astype(jnp.bfloat16)
                low = (rest - middle.astype(jnp.float32)).astype(jnp.bfloat16)
                w_buf[h, step, 0:tokens] = high
                w_buf[h, step, tokens:2 * tokens] = middle
                w_buf[h, step, 2 * tokens:3 * tokens] = low

        def partial(h, q, step):
            y = recv_buf[h, :, :, shift(place[h], step), :, pl.ds(q * quarter, quarter)]
            y = y.astype(jnp.float32).reshape(part_rows, quarter)
            used = used_buf[h, step] > 0.0
            y = jnp.where(jnp.concatenate([used] * (quarter // 128), axis=1), y, 0.0).astype(jnp.bfloat16)
            part = jnp.dot(w_buf[h, step], y, preferred_element_type=jnp.float32)
            return part[0:tokens] + (part[tokens:2 * tokens] + part[2 * tokens:3 * tokens])

        blocks = [(h, q) for q in range(QUARTERS) for h in range(HALVES)]
        for h, q in blocks:
            for e in range(experts):
                first_all(h, e, q).wait_recv()
            far = partial(h, q, 2)
            for way in range(2):
                far_out[h, q, way] = far[way * mid:(way + 1) * mid]
                far_copy(h, q, way).start()
            for way in range(2):
                near_out[h, q, way] = partial(h, q, near_step(way))
                own_copy(h, q, way).start()
        for h, q in blocks:
            for way in range(2):
                far_copy(h, q, way).wait_recv()
                near_out[h, q, way, relay_part(way)] = near_out[h, q, way, relay_part(way)] + far_in[h, q, way]
                sum_copy(h, q, way).start()
            acc[:, pl.ds(h * half + q * quarter, quarter)] = partial(h, q, 0)
        for h, q in blocks:
            for way in range(2):
                own_copy(h, q, way).wait_recv()
                sum_copy(h, q, way).wait_recv()
            cols = pl.ds(h * half + q * quarter, quarter)
            out_ref[:, cols] = (acc[:, cols] + near_in[h, q, 0] + near_in[h, q, 1]).astype(jnp.bfloat16)

        route_all().wait_send()
        for h, q in blocks:
            for e in range(experts):
                first_all(h, e, q).wait_send()
            for way in range(2):
                far_copy(h, q, way).wait_send()
                own_copy(h, q, way).wait_send()
                sum_copy(h, q, way).wait_send()

    return kernel


def solution(mesh):
    outer_devs = mesh.shape["outer"]
    inner_devs = mesh.shape["expert"]
    assert inner_devs == outer_devs * CORES and outer_devs == 4

    def local_step(x_disp, w_gate, w_up, w_down, slot_idx, expert_ids, gate_wts):
        group, experts, capacity, width = x_disp.shape
        ff = w_gate.shape[2]
        tokens, top = slot_idx.shape
        rows = group * capacity
        ring = outer_devs
        peers = inner_devs
        half = width // HALVES
        quarter = half // QUARTERS
        bf16, f32 = jnp.bfloat16, jnp.float32
        hbm = pl.BlockSpec(memory_space=pltpu.HBM)
        dma = pltpu.SemaphoreType.DMA
        return pl.pallas_call(
            make_kernel(ring, experts, capacity, width, ff, tokens, top),
            out_shape=jax.ShapeDtypeStruct((tokens, width), bf16),
            in_specs=[hbm] * 7,
            out_specs=pl.BlockSpec(memory_space=pltpu.VMEM),
            scratch_shapes=[
                pltpu.VMEM((WEIGHT_SLOTS, group, capacity, width), bf16),
                pltpu.VMEM((WEIGHT_SLOTS, width, ff), bf16),
                pltpu.VMEM((WEIGHT_SLOTS, width, ff), bf16),
                pltpu.VMEM((WEIGHT_SLOTS, ff, width), bf16),
                pltpu.VMEM((top, tokens), jnp.int32),
                pltpu.VMEM((top, tokens), jnp.int32),
                pltpu.VMEM((top, tokens), f32),
                pltpu.VMEM((experts, ring, ring, CORES, capacity, width), bf16),
                pltpu.VMEM((HALVES, experts, peers, ring, capacity, half), bf16),
                pltpu.VMEM((HALVES, ring, 2 * top, tokens), f32),
                pltpu.VMEM((HALVES, ring, 3 * tokens, experts * peers * capacity), bf16),
                pltpu.VMEM((HALVES, ring, experts * peers * capacity, 128), f32),
                pltpu.VMEM((HALVES, QUARTERS, 2, tokens // 2, quarter), f32),
                pltpu.VMEM((HALVES, QUARTERS, 2, tokens // 2, quarter), f32),
                pltpu.VMEM((HALVES, QUARTERS, 2, tokens, quarter), f32),
                pltpu.VMEM((HALVES, QUARTERS, 2, tokens, quarter), f32),
                pltpu.VMEM((tokens, width), f32),
                dma((K_PARTS + experts,)),
                dma((K_PARTS + experts,)),
                dma((K_PARTS + experts,)),
                dma((HALVES + experts,)),
                dma((3,)),
                dma((HALVES, experts, QUARTERS)),
                dma((HALVES, experts, QUARTERS)),
                dma((1,)),
                dma((1,)),
                dma((HALVES, QUARTERS, 2)),
                dma((HALVES, QUARTERS, 2)),
                dma((HALVES, QUARTERS, 2)),
                dma((HALVES, QUARTERS, 2)),
                dma((HALVES, QUARTERS, 2)),
                dma((HALVES, QUARTERS, 2)),
            ],
            compiler_params=pltpu.CompilerParams(collective_id=0, has_side_effects=True, vmem_limit_bytes=VMEM_LIMIT),
        )(x_disp, w_gate, w_up, w_down, slot_idx.T, expert_ids.T, gate_wts.T)

    expert_spec = P(("outer", "expert"))
    token_spec = P(("data", "outer", "expert"))
    return jax.shard_map(local_step, mesh=mesh, in_specs=(P("data", ("outer", "expert")), expert_spec, expert_spec, expert_spec, token_spec, token_spec, token_spec), out_specs=token_spec, check_vma=False)
```

time: 164 us -> 58.1 us (0.35)
  the two profiles are of different devices: /device:TPU:96 before, /device:TPU:97 now
where the time goes in v2:
time: 58.1 us; the launch traced here: 58 us
  Pallas kernels  56.1 us (97%)
  local copies, waits for them, and re-layouts  1.88 us (3%)
    pallas_call x1, Pallas kernels, local_step(): pl.pallas_call(make_kernel(ring, experts, capacity, width, ff, tokens, to...  56.1 us
    unnamed x1, local copies, waits for them, and re-layouts  1.88 us

profile of v2, /device:TPU:97, one launch (start us, length us, event | category | flops | bytes accessed | tf_op | source)
XLA Modules:
  0.0 58.0 jit_solution(11369898104347886072)
XLA Ops:
  0.0 56.1 %shard_map.73 = bf16[128,2048]{1,0:T(8,128)(2,1)} custom-call(bf16[32,4,8,2048]{3,2,1,0:T(8,128)(2,1)} %x_hbm.1, bf16[4,2048,768]{2,1,0:T(8,128)(2,1)} %wg_hbm.1, bf16[4,2048,768]{2,1,0:T(8,128)(2,1)} %wu_hbm.1, bf16[4,768,2048]{2,1,0:T(8,128)(2,1)} %wd_hbm.1, s32[8,128]{1,0:T(8,128)} %bitcast.3, s32[8,128]{1,0:T(8,128)} %bitcast.4, f32[8,128]{1,0:T(8,128)} %bitcast.5), custom_call_target="tpu_custom_call" | custom-call | tf_op jit(solution)/shard_map/pallas_call | solution.py:300
  56.1 1.9 %copy.9 = bf16[128,2048]{1,0:T(8,128)(2,1)} copy(bf16[128,2048]{1,0:T(8,128)(2,1)} %shard_map.73) | data formatting | bytes 1048576

commit v3 on v2

--- a/solution.py
+++ b/solution.py
@@ -9,9 +9,9 @@
 CORES = 2
 HALVES = 2
 QUARTERS = 2
-K_PARTS = 2
+K_PARTS = 4
 WEIGHT_SLOTS = 3
-VMEM_LIMIT = 67043328
+VMEM_LIMIT = 62 * 2 ** 20
 BF16_MAX = 3.3895313892515355e38
 
 
@@ -33,6 +33,7 @@
         row = lax.axis_index("outer")
         col = lax.axis_index("expert")
         chip, core = col // CORES, lax.rem(col, CORES)
+        blocks = [(h, q) for q in range(QUARTERS) for h in range(HALVES)]
         place = (row, chip)
         source = (col, row * CORES + core)
 
@@ -118,16 +119,16 @@
                     pltpu.make_async_copy(wg_hbm.at[0, cols], wg_buf.at[0, cols], g_sem.at[k]),
                     pltpu.make_async_copy(wu_hbm.at[0, cols], wu_buf.at[0, cols], u_sem.at[k]))
 
-        def down_part_copy(h):
-            cols = pl.ds(h * half, half)
-            return pltpu.make_async_copy(wd_hbm.at[0, :, cols], wd_buf.at[0, :, cols], d_sem.at[h])
+        def down_part_copy(h, q):
+            cols = pl.ds(h * half + q * quarter, quarter)
+            return pltpu.make_async_copy(wd_hbm.at[0, :, cols], wd_buf.at[0, :, cols], d_sem.at[h * QUARTERS + q])
 
         def weight_copies(e):
             slot = lax.rem(e, WEIGHT_SLOTS)
             return (pltpu.make_async_copy(x_hbm.at[:, e], x_buf.at[slot], x_sem.at[K_PARTS + e]),
                     pltpu.make_async_copy(wg_hbm.at[e], wg_buf.at[slot], g_sem.at[K_PARTS + e]),
                     pltpu.make_async_copy(wu_hbm.at[e], wu_buf.at[slot], u_sem.at[K_PARTS + e]),
-                    pltpu.make_async_copy(wd_hbm.at[e], wd_buf.at[slot], d_sem.at[HALVES + e]))
+                    pltpu.make_async_copy(wd_hbm.at[e], wd_buf.at[slot], d_sem.at[HALVES * QUARTERS + e]))
 
         def token_copies():
             return (pltpu.make_async_copy(slot_hbm, slot_buf, route_sem.at[0]),
@@ -141,18 +142,19 @@
         barrier = pltpu.get_barrier_semaphore()
         for peer in greet:
             pl.semaphore_signal(barrier, inc=1, device_id=peer, device_id_type=MESH_ID)
-        for h in range(HALVES):
-            down_part_copy(h).start()
+        for h, q in blocks:
+            down_part_copy(h, q).start()
         for copy in token_copies():
             copy.start()
         for e in range(1, WEIGHT_SLOTS):
             for copy in weight_copies(e):
                 copy.start()
 
-        def first_send(h, e):
-            for q in range(QUARTERS):
-                for step, flip in hops:
-                    first_copy(h, e, q, step, flip).start()
+        def first_send(h, q, e):
+            for step, flip in hops:
+                first_copy(h, e, q, step, flip).start()
+
+        def keep_own(h, e):
             cols = pl.ds(h * half, half)
             if h == 0:
                 recv_buf[h, e, source[h]] = send_buf[e, :, chip, core, :, cols]
@@ -162,10 +164,10 @@
         def activation(gate_proj, up_proj):
             return (jax.nn.silu(gate_proj) * up_proj).astype(jnp.bfloat16)
 
-        def down_step(e, slot, h, hidden):
-            cols = pl.ds(h * half, half)
+        def down_step(e, slot, start, size, hidden):
+            cols = pl.ds(start, size)
             y = jnp.dot(hidden, wd_buf[slot, :, cols], preferred_element_type=jnp.float32)
-            send_buf[e, :, :, :, :, cols] = y.reshape(ring, ring, CORES, capacity, half).astype(jnp.bfloat16)
+            send_buf[e, :, :, :, :, cols] = y.reshape(ring, ring, CORES, capacity, size).astype(jnp.bfloat16)
 
         gate_proj = up_proj = None
         for k in range(K_PARTS):
@@ -178,12 +180,14 @@
             gate_proj = gate_part if gate_proj is None else gate_proj + gate_part
             up_proj = up_part if up_proj is None else up_proj + up_part
         hidden = activation(gate_proj, up_proj)
+        for h, q in blocks:
+            down_part_copy(h, q).wait()
+            down_step(0, 0, h * half + q * quarter, quarter, hidden)
+            if (h, q) == blocks[0]:
+                pl.semaphore_wait(barrier, len(greet))
+            first_send(h, q, 0)
         for h in range(HALVES):
-            down_part_copy(h).wait()
-            down_step(0, 0, h, hidden)
-            if h == 0:
-                pl.semaphore_wait(barrier, len(greet))
-            first_send(h, 0)
+            keep_own(h, 0)
         for e in range(WEIGHT_SLOTS, experts):
             for copy in weight_copies(e):
                 copy.start()
@@ -212,8 +216,11 @@
             hidden = activation(gate_proj, up_proj)
             down_copy.wait()
             for h in range(HALVES):
-                down_step(e, slot, h, hidden)
-                first_send(h, e)
+                down_step(e, slot, h * half, half, hidden)
+                for q in range(QUARTERS):
+                    first_send(h, q, e)
+            for h in range(HALVES):
+                keep_own(h, e)
 
         route_all().wait_recv()
         line = lax.broadcasted_iota(jnp.int32, (part_rows, tokens), 0)
@@ -244,7 +251,6 @@
             part = jnp.dot(w_buf[h, step], y, preferred_element_type=jnp.float32)
             return part[0:tokens] + (part[tokens:2 * tokens] + part[2 * tokens:3 * tokens])
 
-        blocks = [(h, q) for q in range(QUARTERS) for h in range(HALVES)]
         for h, q in blocks:
             for e in range(experts):
                 first_all(h, e, q).wait_recv()
@@ -299,7 +305,7 @@
         dma = pltpu.SemaphoreType.DMA
         return pl.pallas_call(
             make_kernel(ring, experts, capacity, width, ff, tokens, top),
-            out_shape=jax.ShapeDtypeStruct((tokens, width), bf16),
+            out_shape=pltpu.VMEM((tokens, width), bf16),
             in_specs=[hbm] * 7,
             out_specs=pl.BlockSpec(memory_space=pltpu.VMEM),
             scratch_shapes=[
@@ -323,7 +329,7 @@
                 dma((K_PARTS + experts,)),
                 dma((K_PARTS + experts,)),
                 dma((K_PARTS + experts,)),
-                dma((HALVES + experts,)),
+                dma((HALVES * QUARTERS + experts,)),
                 dma((3,)),
                 dma((HALVES, experts, QUARTERS)),
                 dma((HALVES, experts, QUARTERS)),

time: 58.1 us -> 54.9 us (0.945)
  Pallas kernels: 56.1 us -> 54 us
  local copies, waits for them, and re-layouts: 1.88 us -> 0.8 us
    pallas_call x1, Pallas kernels: 56.1 us -> 54 us  [local_step(): pl.pallas_call(make_kernel(ring, experts, capacity, width, ff, tokens, to...]
    unnamed x1, local copies, waits for them, and re-layouts: 1.88 us -> 0.8 us
where the time goes in v3:
time: 54.9 us; the launch traced here: 54.8 us
  Pallas kernels  54 us (98%)
  local copies, waits for them, and re-layouts  0.8 us (1%)
    pallas_call x1, Pallas kernels, local_step(): pl.pallas_call(make_kernel(ring, experts, capacity, width, ff, tokens, to...  54 us

profile of v3, /device:TPU:97, one launch (start us, length us, event | category | flops | bytes accessed | tf_op | source)
XLA Modules:
  0.0 54.8 jit_solution(13975759631976329560)
XLA Ops:
  0.0 54.0 %shard_map.73 = bf16[128,2048]{1,0:T(8,128)(2,1)S(1)} custom-call(bf16[32,4,8,2048]{3,2,1,0:T(8,128)(2,1)} %x_hbm.1, bf16[4,2048,768]{2,1,0:T(8,128)(2,1)} %wg_hbm.1, bf16[4,2048,768]{2,1,0:T(8,128)(2,1)} %wu_hbm.1, bf16[4,768,2048]{2,1,0:T(8,128)(2,1)} %wd_hbm.1, s32[8,128]{1,0:T(8,128)} %bitcast.3, s32[8,128]{1,0:T(8,128)} %bitcast.4, f32[8,128]{1,0:T(8,128)} %bitcast.5), custom_call_target="tpu_custom_call" | custom-call | tf_op jit(solution)/shard_map/pallas_call | solution.py:306
  54.0 0.8 %copy.9 = bf16[128,2048]{1,0:T(8,128)(2,1)} copy(bf16[128,2048]{1,0:T(8,128)(2,1)S(1)} %shard_map.73) | data formatting | bytes 1048576

commit v4 on v3

--- a/solution.py
+++ b/solution.py
@@ -28,8 +28,8 @@
     def kernel(x_hbm, wg_hbm, wu_hbm, wd_hbm, slot_hbm, eid_hbm, gate_hbm, out_ref,
                x_buf, wg_buf, wu_buf, wd_buf, slot_buf, eid_buf, gate_buf, send_buf, recv_buf,
                routes, w_buf, used_buf, far_out, far_in, near_out, near_in, acc,
-               x_sem, g_sem, u_sem, d_sem, route_sem, p1_send, p1_recv, rt_send, rt_recv,
-               far_send, far_recv, own_send, own_recv, sum_send, sum_recv):
+               part_sem, down_sem, weight_sem, token_sem, first_out, first_in, route_out, route_in,
+               far_sent, far_here, near_sent, own_here, sum_here):
         row = lax.axis_index("outer")
         col = lax.axis_index("expert")
         chip, core = col // CORES, lax.rem(col, CORES)
@@ -65,25 +65,31 @@
             return pltpu.make_async_remote_copy(
                 src_ref=rows_for(h, e, to, other, pl.ds(h * half + q * quarter, quarter)),
                 dst_ref=recv_buf.at[h, e, source[h], :, :, pl.ds(q * quarter, quarter)],
-                send_sem=p1_send.at[h, e, q], recv_sem=p1_recv.at[h, e, q],
+                send_sem=first_out.at[0], recv_sem=first_in.at[h, q],
                 device_id=peer, device_id_type=MESH_ID)
 
-        def first_all(h, e, q):
-            ref = recv_buf.at[h, e, pl.ds(0, peers - 1), :, :, pl.ds(q * quarter, quarter)]
-            return pltpu.make_async_remote_copy(
-                src_ref=ref, dst_ref=ref, send_sem=p1_send.at[h, e, q], recv_sem=p1_recv.at[h, e, q],
-                device_id=ring_peer(h, 1), device_id_type=MESH_ID)
+        def whole(ref, sent, here):
+            return pltpu.make_async_remote_copy(
+                src_ref=ref, dst_ref=ref, send_sem=sent, recv_sem=here,
+                device_id=ring_peer(0, 1), device_id_type=MESH_ID)
+
+        def first_here(h, q):
+            ref = recv_buf.at[h, :, pl.ds(0, peers - 1), :, :, pl.ds(q * quarter, quarter)]
+            return whole(ref, first_out.at[0], first_in.at[h, q])
+
+        def first_sent():
+            return whole(recv_buf.at[:, :, pl.ds(0, peers - 1)], first_out.at[0], first_in.at[0, 0])
 
         def route_copy(h, step):
             return pltpu.make_async_remote_copy(
                 src_ref=routes.at[h, 0], dst_ref=routes.at[h, ring - step],
-                send_sem=rt_send.at[0], recv_sem=rt_recv.at[0],
+                send_sem=route_out.at[0], recv_sem=route_in.at[0],
                 device_id=ring_peer(h, step), device_id_type=MESH_ID)
 
         def route_all():
             ref = routes.at[:, pl.ds(1, ring - 1)]
             return pltpu.make_async_remote_copy(
-                src_ref=ref, dst_ref=ref, send_sem=rt_send.at[0], recv_sem=rt_recv.at[0],
+                src_ref=ref, dst_ref=ref, send_sem=route_out.at[0], recv_sem=route_in.at[0],
                 device_id=ring_peer(0, 1), device_id_type=MESH_ID)
 
         def near_step(way):
@@ -98,42 +104,45 @@
         def far_copy(h, q, way):
             return pltpu.make_async_remote_copy(
                 src_ref=far_out.at[h, q, way], dst_ref=far_in.at[h, q, way],
-                send_sem=far_send.at[h, q, way], recv_sem=far_recv.at[h, q, way],
+                send_sem=far_sent.at[0], recv_sem=far_here.at[h, q, way],
                 device_id=ring_peer(h, near_step(way)), device_id_type=MESH_ID)
 
         def own_copy(h, q, way):
             return pltpu.make_async_remote_copy(
                 src_ref=near_out.at[h, q, way, own_part(way)], dst_ref=near_in.at[h, q, way, own_part(way)],
-                send_sem=own_send.at[h, q, way], recv_sem=own_recv.at[h, q, way],
+                send_sem=near_sent.at[0], recv_sem=own_here.at[h, q],
                 device_id=ring_peer(h, near_step(way)), device_id_type=MESH_ID)
 
         def sum_copy(h, q, way):
             return pltpu.make_async_remote_copy(
                 src_ref=near_out.at[h, q, way, relay_part(way)], dst_ref=near_in.at[h, q, way, relay_part(way)],
-                send_sem=sum_send.at[h, q, way], recv_sem=sum_recv.at[h, q, way],
+                send_sem=near_sent.at[0], recv_sem=sum_here.at[h, q],
                 device_id=ring_peer(h, near_step(way)), device_id_type=MESH_ID)
+
+        def both_ways(h, q, here):
+            return whole(near_in.at[h, q, :, pl.ds(0, mid)], near_sent.at[0], here.at[h, q])
 
         def part_copies(k):
             cols = pl.ds(k * k_size, k_size)
-            return (pltpu.make_async_copy(x_hbm.at[:, 0, :, cols], x_buf.at[0, :, :, cols], x_sem.at[k]),
-                    pltpu.make_async_copy(wg_hbm.at[0, cols], wg_buf.at[0, cols], g_sem.at[k]),
-                    pltpu.make_async_copy(wu_hbm.at[0, cols], wu_buf.at[0, cols], u_sem.at[k]))
+            return (pltpu.make_async_copy(x_hbm.at[:, 0, :, cols], x_buf.at[0, :, :, cols], part_sem.at[0, k]),
+                    pltpu.make_async_copy(wg_hbm.at[0, cols], wg_buf.at[0, cols], part_sem.at[1, k]),
+                    pltpu.make_async_copy(wu_hbm.at[0, cols], wu_buf.at[0, cols], part_sem.at[2, k]))
 
         def down_part_copy(h, q):
             cols = pl.ds(h * half + q * quarter, quarter)
-            return pltpu.make_async_copy(wd_hbm.at[0, :, cols], wd_buf.at[0, :, cols], d_sem.at[h * QUARTERS + q])
+            return pltpu.make_async_copy(wd_hbm.at[0, :, cols], wd_buf.at[0, :, cols], down_sem.at[h, q])
 
         def weight_copies(e):
             slot = lax.rem(e, WEIGHT_SLOTS)
-            return (pltpu.make_async_copy(x_hbm.at[:, e], x_buf.at[slot], x_sem.at[K_PARTS + e]),
-                    pltpu.make_async_copy(wg_hbm.at[e], wg_buf.at[slot], g_sem.at[K_PARTS + e]),
-                    pltpu.make_async_copy(wu_hbm.at[e], wu_buf.at[slot], u_sem.at[K_PARTS + e]),
-                    pltpu.make_async_copy(wd_hbm.at[e], wd_buf.at[slot], d_sem.at[HALVES * QUARTERS + e]))
+            return (pltpu.make_async_copy(x_hbm.at[:, e], x_buf.at[slot], weight_sem.at[0, e - 1]),
+                    pltpu.make_async_copy(wg_hbm.at[e], wg_buf.at[slot], weight_sem.at[1, e - 1]),
+                    pltpu.make_async_copy(wu_hbm.at[e], wu_buf.at[slot], weight_sem.at[2, e - 1]),
+                    pltpu.make_async_copy(wd_hbm.at[e], wd_buf.at[slot], weight_sem.at[3, e - 1]))
 
         def token_copies():
-            return (pltpu.make_async_copy(slot_hbm, slot_buf, route_sem.at[0]),
-                    pltpu.make_async_copy(eid_hbm, eid_buf, route_sem.at[1]),
-                    pltpu.make_async_copy(gate_hbm, gate_buf, route_sem.at[2]))
+            return (pltpu.make_async_copy(slot_hbm, slot_buf, token_sem.at[0]),
+                    pltpu.make_async_copy(eid_hbm, eid_buf, token_sem.at[1]),
+                    pltpu.make_async_copy(gate_hbm, gate_buf, token_sem.at[2]))
 
         for k in range(K_PARTS):
             for copy in part_copies(k):
@@ -146,9 +155,8 @@
             down_part_copy(h, q).start()
         for copy in token_copies():
             copy.start()
-        for e in range(1, WEIGHT_SLOTS):
-            for copy in weight_copies(e):
-                copy.start()
+        for copy in weight_copies(1):
+            copy.start()
 
         def first_send(h, q, e):
             for step, flip in hops:
@@ -185,12 +193,12 @@
             down_step(0, 0, h * half + q * quarter, quarter, hidden)
             if (h, q) == blocks[0]:
                 pl.semaphore_wait(barrier, len(greet))
+            if (h, q) == blocks[0]:
+                for copy in weight_copies(2):
+                    copy.start()
             first_send(h, q, 0)
         for h in range(HALVES):
             keep_own(h, 0)
-        for e in range(WEIGHT_SLOTS, experts):
-            for copy in weight_copies(e):
-                copy.start()
 
         for copy in token_copies():
             copy.wait()
@@ -215,6 +223,11 @@
             up_proj = jnp.dot(x_rows, wu_buf[slot], preferred_element_type=jnp.float32)
             hidden = activation(gate_proj, up_proj)
             down_copy.wait()
+
+            @pl.when(e + 2 < experts)
+            def _():
+                for copy in weight_copies(e + 2):
+                    copy.start()
             for h in range(HALVES):
                 down_step(e, slot, h * half, half, hidden)
                 for q in range(QUARTERS):
@@ -251,16 +264,20 @@
             part = jnp.dot(w_buf[h, step], y, preferred_element_type=jnp.float32)
             return part[0:tokens] + (part[tokens:2 * tokens] + part[2 * tokens:3 * tokens])
 
-        for h, q in blocks:
-            for e in range(experts):
-                first_all(h, e, q).wait_recv()
+        late_core = core == 0
+        for h, q in blocks:
+            first_here(h, q).wait_recv()
             far = partial(h, q, 2)
             for way in range(2):
                 far_out[h, q, way] = far[way * mid:(way + 1) * mid]
                 far_copy(h, q, way).start()
             for way in range(2):
                 near_out[h, q, way] = partial(h, q, near_step(way))
-                own_copy(h, q, way).start()
+
+            @pl.when(jnp.logical_not(late_core))
+            def _():
+                for way in range(2):
+                    own_copy(h, q, way).start()
         for h, q in blocks:
             for way in range(2):
                 far_copy(h, q, way).wait_recv()
@@ -268,20 +285,23 @@
                 sum_copy(h, q, way).start()
             acc[:, pl.ds(h * half + q * quarter, quarter)] = partial(h, q, 0)
         for h, q in blocks:
-            for way in range(2):
-                own_copy(h, q, way).wait_recv()
-                sum_copy(h, q, way).wait_recv()
+            both_ways(h, q, sum_here).wait_recv()
+
+            if q == QUARTERS - 1:
+                @pl.when(late_core)
+                def _():
+                    for part in range(QUARTERS):
+                        for way in range(2):
+                            own_copy(h, part, way).start()
+        for h, q in blocks:
+            both_ways(h, q, own_here).wait_recv()
             cols = pl.ds(h * half + q * quarter, quarter)
             out_ref[:, cols] = (acc[:, cols] + near_in[h, q, 0] + near_in[h, q, 1]).astype(jnp.bfloat16)
 
         route_all().wait_send()
-        for h, q in blocks:
-            for e in range(experts):
-                first_all(h, e, q).wait_send()
-            for way in range(2):
-                far_copy(h, q, way).wait_send()
-                own_copy(h, q, way).wait_send()
-                sum_copy(h, q, way).wait_send()
+        first_sent().wait_send()
+        whole(far_out, far_sent.at[0], far_here.at[0, 0, 0]).wait_send()
+        whole(near_out, near_sent.at[0], own_here.at[0, 0]).wait_send()
 
     return kernel
 
@@ -326,21 +346,19 @@
                 pltpu.VMEM((HALVES, QUARTERS, 2, tokens, quarter), f32),
                 pltpu.VMEM((HALVES, QUARTERS, 2, tokens, quarter), f32),
                 pltpu.VMEM((tokens, width), f32),
-                dma((K_PARTS + experts,)),
-                dma((K_PARTS + experts,)),
-                dma((K_PARTS + experts,)),
-                dma((HALVES * QUARTERS + experts,)),
+                dma((3, K_PARTS)),
+                dma((HALVES, QUARTERS)),
+                dma((4, experts - 1)),
                 dma((3,)),
-                dma((HALVES, experts, QUARTERS)),
-                dma((HALVES, experts, QUARTERS)),
+                dma((1,)),
+                dma((HALVES, QUARTERS)),
+                dma((1,)),
                 dma((1,)),
                 dma((1,)),
                 dma((HALVES, QUARTERS, 2)),
-                dma((HALVES, QUARTERS, 2)),
-                dma((HALVES, QUARTERS, 2)),
-                dma((HALVES, QUARTERS, 2)),
-                dma((HALVES, QUARTERS, 2)),
-                dma((HALVES, QUARTERS, 2)),
+                dma((1,)),
+                dma((HALVES, QUARTERS)),
+                dma((HALVES, QUARTERS)),
             ],
             compiler_params=pltpu.CompilerParams(collective_id=0, has_side_effects=True, vmem_limit_bytes=VMEM_LIMIT),
         )(x_disp, w_gate, w_up, w_down, slot_idx.T, expert_ids.T, gate_wts.T)

time: 54.9 us -> 53 us (0.965)
  the two profiles are of different devices: /device:TPU:97 before, /device:TPU:96 now
where the time goes in v4:
time: 53 us; the launch traced here: 52.9 us
  Pallas kernels  52.1 us (98%)
  local copies, waits for them, and re-layouts  0.8 us (2%)
    pallas_call x1, Pallas kernels, local_step(): pl.pallas_call(make_kernel(ring, experts, capacity, width, ff, tokens, to...  52.1 us

profile of v4, /device:TPU:96, one launch (start us, length us, event | category | flops | bytes accessed | tf_op | source)
XLA Modules:
  0.0 52.9 jit_solution(2163075842983467208)
XLA Ops:
  0.0 52.1 %shard_map.73 = bf16[128,2048]{1,0:T(8,128)(2,1)S(1)} custom-call(bf16[32,4,8,2048]{3,2,1,0:T(8,128)(2,1)} %x_hbm.1, bf16[4,2048,768]{2,1,0:T(8,128)(2,1)} %wg_hbm.1, bf16[4,2048,768]{2,1,0:T(8,128)(2,1)} %wu_hbm.1, bf16[4,768,2048]{2,1,0:T(8,128)(2,1)} %wd_hbm.1, s32[8,128]{1,0:T(8,128)} %bitcast.3, s32[8,128]{1,0:T(8,128)} %bitcast.4, f32[8,128]{1,0:T(8,128)} %bitcast.5), custom_call_target="tpu_custom_call" | custom-call | tf_op jit(solution)/shard_map/pallas_call | solution.py:326
  52.1 0.8 %copy.9 = bf16[128,2048]{1,0:T(8,128)(2,1)} copy(bf16[128,2048]{1,0:T(8,128)(2,1)S(1)} %shard_map.73) | data formatting | bytes 1048576

commit v5 on v4

v5 whole, which is shorter than its diff:
```python
import jax
import jax.numpy as jnp
from jax import lax
from jax.experimental import pallas as pl
from jax.experimental.pallas import tpu as pltpu
from jax.sharding import PartitionSpec as P

MESH_ID = pl.DeviceIdType.MESH
CORES = 2
BLOCKS = ((0, 0, 512), (1, 1024, 512), (0, 512, 512), (1, 1536, 512))
LATE = ((1, 0), (1, 1), (2, 2), (3, 3))
HALVES = 2
DOWN_PARTS = 2
K_SIZES = (512, 512, 512, 512)
K_PARTS = len(K_SIZES)
FIRST_ORDER = (0, 1, 2, 3)
WEIGHT_SLOTS = 3
VMEM_LIMIT = 62 * 2 ** 20
BF16_MAX = 3.3895313892515355e38


def make_kernel(ring, experts, capacity, width, ff, tokens, top):
    peers = ring * CORES
    group = ring * peers
    rows = group * capacity
    part_rows = experts * peers * capacity
    n_blocks = len(BLOCKS)
    down_size = width // DOWN_PARTS
    mid = tokens // 2

    def kernel(x_hbm, wg_hbm, wu_hbm, wd_hbm, slot_hbm, eid_hbm, gate_hbm, out_ref,
               x_buf, wg_buf, wu_buf, wd_buf, slot_buf, eid_buf, gate_buf, send_buf, recv_buf,
               routes, w_buf, used_buf, far_out, far_in, near_out, near_in, acc,
               part_sem, down_sem, weight_sem, token_sem, first_out, first_in, route_out, route_in,
               far_sent, far_here, near_sent, own_here, sum_here):
        row = lax.axis_index("outer")
        col = lax.axis_index("expert")
        chip, core = col // CORES, lax.rem(col, CORES)
        def columns(b):
            return pl.ds(BLOCKS[b][1], BLOCKS[b][2])

        place = (row, chip)
        source = (col, row * CORES + core)

        def shift(start, step):
            return lax.rem(start + step, ring)

        def ring_peer(h, step):
            if h == 0:
                return {"outer": shift(row, step), "expert": col}
            return {"outer": row, "expert": shift(chip, step) * CORES + core}

        def first_peer(h, step, flip):
            other = lax.rem(core + flip, CORES)
            if h == 0:
                to = shift(chip, step)
                return {"outer": row, "expert": to * CORES + other}, to, other
            to = shift(row, step)
            return {"outer": to, "expert": chip * CORES + other}, to, other

        def rows_for(h, e, to, other, cols):
            if h == 0:
                return send_buf.at[e, :, to, other, :, cols]
            return send_buf.at[e, to, :, other, :, cols]

        hops = [(2, 0), (2, 1), (1, 0), (ring - 1, 0), (1, 1), (ring - 1, 1), (0, 1)]

        def first_copy(b, e, step, flip):
            h = BLOCKS[b][0]
            peer, to, other = first_peer(h, step, flip)
            return pltpu.make_async_remote_copy(
                src_ref=rows_for(h, e, to, other, columns(b)),
                dst_ref=recv_buf.at[e, source[h], :, :, columns(b)],
                send_sem=first_out.at[0], recv_sem=first_in.at[b],
                device_id=peer, device_id_type=MESH_ID)

        def whole(ref, sent, here):
            return pltpu.make_async_remote_copy(
                src_ref=ref, dst_ref=ref, send_sem=sent, recv_sem=here,
                device_id=ring_peer(0, 1), device_id_type=MESH_ID)

        def first_here(b):
            return whole(recv_buf.at[:, pl.ds(0, peers - 1), :, :, columns(b)], first_out.at[0], first_in.at[b])

        def first_sent():
            return whole(recv_buf.at[:, pl.ds(0, peers - 1)], first_out.at[0], first_in.at[0])

        def route_copy(h, step):
            return pltpu.make_async_remote_copy(
                src_ref=routes.at[h, 0], dst_ref=routes.at[h, ring - step],
                send_sem=route_out.at[0], recv_sem=route_in.at[0],
                device_id=ring_peer(h, step), device_id_type=MESH_ID)

        def route_all():
            ref = routes.at[:, pl.ds(1, ring - 1)]
            return pltpu.make_async_remote_copy(
                src_ref=ref, dst_ref=ref, send_sem=route_out.at[0], recv_sem=route_in.at[0],
                device_id=ring_peer(0, 1), device_id_type=MESH_ID)

        def near_step(way):
            return 1 if way == 0 else ring - 1

        def relay_part(way):
            return pl.ds(way * mid, mid)

        def own_part(way):
            return pl.ds((1 - way) * mid, mid)

        def ring_copy(b, way, src, dst, sent, here):
            return pltpu.make_async_remote_copy(
                src_ref=src, dst_ref=dst, send_sem=sent.at[0], recv_sem=here,
                device_id=ring_peer(BLOCKS[b][0], near_step(way)), device_id_type=MESH_ID)

        def far_copy(b, way):
            cols = columns(b)
            return ring_copy(b, way, far_out.at[way, :, cols], far_in.at[way, :, cols], far_sent, far_here.at[b, way])

        def own_copy(b, way):
            cols, part = columns(b), own_part(way)
            return ring_copy(b, way, near_out.at[way, part, cols], near_in.at[way, part, cols], near_sent, own_here.at[b])

        def sum_copy(b, way):
            cols, part = columns(b), relay_part(way)
            return ring_copy(b, way, near_out.at[way, part, cols], near_in.at[way, part, cols], near_sent, sum_here.at[b])

        def both_ways(b, here):
            return whole(near_in.at[:, pl.ds(0, mid), columns(b)], near_sent.at[0], here.at[b])

        def k_slice(k):
            return pl.ds(sum(K_SIZES[:k]), K_SIZES[k])

        def part_copies(k):
            cols = k_slice(k)
            return (pltpu.make_async_copy(x_hbm.at[:, 0, :, cols], x_buf.at[0, :, :, cols], part_sem.at[0, k]),
                    pltpu.make_async_copy(wg_hbm.at[0, cols], wg_buf.at[0, cols], part_sem.at[1, k]),
                    pltpu.make_async_copy(wu_hbm.at[0, cols], wu_buf.at[0, cols], part_sem.at[2, k]))

        def down_part_copy(b):
            cols = columns(b)
            return pltpu.make_async_copy(wd_hbm.at[0, :, cols], wd_buf.at[0, :, cols], down_sem.at[b])

        def weight_copies(e):
            slot = lax.rem(e, WEIGHT_SLOTS)
            return (pltpu.make_async_copy(x_hbm.at[:, e], x_buf.at[slot], weight_sem.at[0, lax.rem(e, 2)]),
                    pltpu.make_async_copy(wg_hbm.at[e], wg_buf.at[slot], weight_sem.at[1, lax.rem(e, 2)]),
                    pltpu.make_async_copy(wu_hbm.at[e], wu_buf.at[slot], weight_sem.at[2, lax.rem(e, 2)]),
                    pltpu.make_async_copy(wd_hbm.at[e], wd_buf.at[slot], weight_sem.at[3, lax.rem(e, 2)]))

        def token_copies():
            return (pltpu.make_async_copy(slot_hbm, slot_buf, token_sem.at[0]),
                    pltpu.make_async_copy(eid_hbm, eid_buf, token_sem.at[1]),
                    pltpu.make_async_copy(gate_hbm, gate_buf, token_sem.at[2]))

        for k in range(K_PARTS):
            for copy in part_copies(k):
                copy.start()
        greet = [first_peer(h, step, flip)[0] for h in range(HALVES) for step, flip in hops[:-1]] + [first_peer(0, 0, 1)[0]]
        barrier = pltpu.get_barrier_semaphore()
        for peer in greet:
            pl.semaphore_signal(barrier, inc=1, device_id=peer, device_id_type=MESH_ID)
        for b in FIRST_ORDER:
            down_part_copy(b).start()
        for copy in token_copies():
            copy.start()
        for copy in weight_copies(1):
            copy.start()

        def first_send(b, e):
            for step, flip in hops:
                first_copy(b, e, step, flip).start()

        def keep_own(e):
            for b in range(n_blocks):
                cols = columns(b)
                if BLOCKS[b][0] == 0:
                    recv_buf[e, source[0], :, :, cols] = send_buf[e, :, chip, core, :, cols]
                else:
                    recv_buf[e, source[1], :, :, cols] = send_buf[e, row, :, core, :, cols]

        def activation(gate_proj, up_proj):
            return (jax.nn.silu(gate_proj) * up_proj).astype(jnp.bfloat16)

        def down_step(e, slot, start, size, hidden):
            cols = pl.ds(start, size)
            y = jnp.dot(hidden, wd_buf[slot, :, cols], preferred_element_type=jnp.float32)
            send_buf[e, :, :, :, :, cols] = y.reshape(ring, ring, CORES, capacity, size).astype(jnp.bfloat16)

        gate_proj = up_proj = None
        for k in range(K_PARTS):
            for copy in part_copies(k):
                copy.wait()
            cols = k_slice(k)
            x_rows = x_buf[0, :, :, cols].reshape(rows, K_SIZES[k])
            gate_part = jnp.dot(x_rows, wg_buf[0, cols], preferred_element_type=jnp.float32)
            up_part = jnp.dot(x_rows, wu_buf[0, cols], preferred_element_type=jnp.float32)
            gate_proj = gate_part if gate_proj is None else gate_proj + gate_part
            up_proj = up_part if up_proj is None else up_proj + up_part
        hidden = activation(gate_proj, up_proj)
        for b in FIRST_ORDER:
            down_part_copy(b).wait()
            down_step(0, 0, BLOCKS[b][1], BLOCKS[b][2], hidden)
            if b == FIRST_ORDER[0]:
                pl.semaphore_wait(barrier, len(greet))
                for copy in weight_copies(2):
                    copy.start()
            first_send(b, 0)
        keep_own(0)

        for copy in token_copies():
            copy.wait()
        slots = slot_buf[...]
        keys = jnp.where(slots >= 0, eid_buf[...] * capacity + slots, -1).astype(jnp.float32)
        for h in range(HALVES):
            routes[h, 0, 0:top] = keys
            routes[h, 0, top:2 * top] = gate_buf[...]
        for h in range(HALVES):
            for step in range(1, ring):
                route_copy(h, step).start()

        @pl.loop(1, experts)
        def _(e):
            slot = lax.rem(e, WEIGHT_SLOTS)
            x_copy, gate_copy, up_copy, down_copy = weight_copies(e)
            x_copy.wait()
            x_rows = x_buf[slot].reshape(rows, width)
            gate_copy.wait()
            gate_proj = jnp.dot(x_rows, wg_buf[slot], preferred_element_type=jnp.float32)
            up_copy.wait()
            up_proj = jnp.dot(x_rows, wu_buf[slot], preferred_element_type=jnp.float32)
            hidden = activation(gate_proj, up_proj)
            down_copy.wait()

            @pl.when(e + 2 < experts)
            def _():
                for copy in weight_copies(e + 2):
                    copy.start()
            for part in range(DOWN_PARTS):
                down_step(e, slot, part * down_size, down_size, hidden)
                for b in range(n_blocks // 2):
                    if (BLOCKS[b][1] + BLOCKS[b][2] - 1) // down_size == part:
                        first_send(b, e)

            @pl.when(e == experts - 1)
            def _():
                for b in range(n_blocks // 2, n_blocks):
                    first_send(b, e - 1)

            @pl.when(e != experts - 2)
            def _():
                for b in range(n_blocks // 2, n_blocks):
                    first_send(b, e)
            keep_own(e)

        route_all().wait_recv()
        line = lax.broadcasted_iota(jnp.int32, (part_rows, tokens), 0)
        local = line // (peers * capacity)
        src = lax.rem(line // capacity, peers)
        device = (row * peers + src, (src // CORES) * peers + chip * CORES + lax.rem(src, CORES))
        for h in range(HALVES):
            row_key = ((device[h] * experts + local) * capacity + lax.rem(line, capacity)).astype(jnp.float32)
            for step in range(ring):
                weight = jnp.zeros((part_rows, tokens), jnp.float32)
                for j in range(top):
                    weight = weight + jnp.where(row_key == routes[h, step, j:j + 1], routes[h, step, top + j:top + j + 1], 0.0)
                used_buf[h, step] = jnp.broadcast_to(jnp.max(weight, axis=1, keepdims=True), (part_rows, 128))
                weight = weight.T
                high = jnp.minimum(weight, BF16_MAX).astype(jnp.bfloat16)
                rest = weight - high.astype(jnp.float32)
                middle = rest.astype(jnp.bfloat16)
                low = (rest - middle.astype(jnp.float32)).astype(jnp.bfloat16)
                w_buf[h, step, 0:tokens] = high
                w_buf[h, step, tokens:2 * tokens] = middle
                w_buf[h, step, 2 * tokens:3 * tokens] = low

        def partial(b, step):
            h, _, size = BLOCKS[b]
            y = recv_buf[:, :, shift(place[h], step), :, columns(b)]
            y = y.astype(jnp.float32).reshape(part_rows, size)
            used = used_buf[h, step] > 0.0
            y = jnp.where(jnp.concatenate([used] * (size // 128), axis=1), y, 0.0).astype(jnp.bfloat16)
            part = jnp.dot(w_buf[h, step], y, preferred_element_type=jnp.float32)
            return part[0:tokens] + (part[tokens:2 * tokens] + part[2 * tokens:3 * tokens])

        late_core = core == 0
        for b in range(n_blocks):
            first_here(b).wait_recv()
            far = partial(b, 2)
            for way in range(2):
                far_out[way, :, columns(b)] = far[way * mid:(way + 1) * mid]
                far_copy(b, way).start()
            for way in range(2):
                near_out[way, :, columns(b)] = partial(b, near_step(way))

            @pl.when(jnp.logical_not(late_core))
            def _():
                for way in range(2):
                    own_copy(b, way).start()
        for b in range(n_blocks):
            for way in range(2):
                far_copy(b, way).wait_recv()
                part, cols = relay_part(way), columns(b)
                near_out[way, part, cols] = near_out[way, part, cols] + far_in[way, :, cols]
                sum_copy(b, way).start()
            acc[:, columns(b)] = partial(b, 0)
        for b in range(n_blocks):
            both_ways(b, sum_here).wait_recv()
            late = [n for trigger, n in LATE if trigger == b]
            if late:
                @pl.when(late_core)
                def _():
                    for n in late:
                        for way in range(2):
                            own_copy(n, way).start()
        for b in range(n_blocks):
            both_ways(b, own_here).wait_recv()
            cols = columns(b)
            out_ref[:, cols] = (acc[:, cols] + near_in[0, :, cols] + near_in[1, :, cols]).astype(jnp.bfloat16)

        route_all().wait_send()
        first_sent().wait_send()
        whole(far_out, far_sent.at[0], far_here.at[0, 0]).wait_send()
        whole(near_out, near_sent.at[0], own_here.at[0]).wait_send()

    return kernel


def solution(mesh):
    outer_devs = mesh.shape["outer"]
    inner_devs = mesh.shape["expert"]
    assert inner_devs == outer_devs * CORES and outer_devs == 4

    def local_step(x_disp, w_gate, w_up, w_down, slot_idx, expert_ids, gate_wts):
        group, experts, capacity, width = x_disp.shape
        ff = w_gate.shape[2]
        tokens, top = slot_idx.shape
        rows = group * capacity
        ring = outer_devs
        peers = inner_devs
        n_blocks = len(BLOCKS)
        bf16, f32 = jnp.bfloat16, jnp.float32
        hbm = pl.BlockSpec(memory_space=pltpu.HBM)
        dma = pltpu.SemaphoreType.DMA
        return pl.pallas_call(
            make_kernel(ring, experts, capacity, width, ff, tokens, top),
            out_shape=pltpu.VMEM((tokens, width), bf16),
            in_specs=[hbm] * 7,
            out_specs=pl.BlockSpec(memory_space=pltpu.VMEM),
            scratch_shapes=[
                pltpu.VMEM((WEIGHT_SLOTS, group, capacity, width), bf16),
                pltpu.VMEM((WEIGHT_SLOTS, width, ff), bf16),
                pltpu.VMEM((WEIGHT_SLOTS, width, ff), bf16),
                pltpu.VMEM((WEIGHT_SLOTS, ff, width), bf16),
                pltpu.VMEM((top, tokens), jnp.int32),
                pltpu.VMEM((top, tokens), jnp.int32),
                pltpu.VMEM((top, tokens), f32),
                pltpu.VMEM((experts, ring, ring, CORES, capacity, width), bf16),
                pltpu.VMEM((experts, peers, ring, capacity, width), bf16),
                pltpu.VMEM((HALVES, ring, 2 * top, tokens), f32),
                pltpu.VMEM((HALVES, ring, 3 * tokens, experts * peers * capacity), bf16),
                pltpu.VMEM((HALVES, ring, experts * peers * capacity, 128), f32),
                pltpu.VMEM((2, tokens // 2, width), f32),
                pltpu.VMEM((2, tokens // 2, width), f32),
                pltpu.VMEM((2, tokens, width), f32),
                pltpu.VMEM((2, tokens, width), f32),
                pltpu.VMEM((tokens, width), f32),
                dma((3, K_PARTS)),
                dma((n_blocks,)),
                dma((4, 2)),
                dma((3,)),
                dma((1,)),
                dma((n_blocks,)),
                dma((1,)),
                dma((1,)),
                dma((1,)),
                dma((n_blocks, 2)),
                dma((1,)),
                dma((n_blocks,)),
                dma((n_blocks,)),
            ],
            compiler_params=pltpu.CompilerParams(collective_id=0, has_side_effects=True, vmem_limit_bytes=VMEM_LIMIT),
        )(x_disp, w_gate, w_up, w_down, slot_idx.T, expert_ids.T, gate_wts.T)

    expert_spec = P(("outer", "expert"))
    token_spec = P(("data", "outer", "expert"))
    return jax.shard_map(local_step, mesh=mesh, in_specs=(P("data", ("outer", "expert")), expert_spec, expert_spec, expert_spec, token_spec, token_spec, token_spec), out_specs=token_spec, check_vma=False)
```

time: 53 us -> 51.1 us (0.964)
  Pallas kernels: 52.1 us -> 50.3 us
    pallas_call x1, Pallas kernels: 52.1 us -> 50.3 us  [local_step(): pl.pallas_call(make_kernel(ring, experts, capacity, width, ff, tokens, to...]
where the time goes in v5:
time: 51.1 us
  Pallas kernels  50.3 us (98%)
  local copies, waits for them, and re-layouts  0.8 us (2%)
    pallas_call x1, Pallas kernels, local_step(): pl.pallas_call(make_kernel(ring, experts, capacity, width, ff, tokens, to...  50.3 us

profile of v5, /device:TPU:96, one launch (start us, length us, event | category | flops | bytes accessed | tf_op | source)
XLA Modules:
  0.0 51.1 jit_solution(205973683146028792)
XLA Ops:
  0.0 50.3 %shard_map.73 = bf16[128,2048]{1,0:T(8,128)(2,1)S(1)} custom-call(bf16[32,4,8,2048]{3,2,1,0:T(8,128)(2,1)} %x_hbm.1, bf16[4,2048,768]{2,1,0:T(8,128)(2,1)} %wg_hbm.1, bf16[4,2048,768]{2,1,0:T(8,128)(2,1)} %wu_hbm.1, bf16[4,768,2048]{2,1,0:T(8,128)(2,1)} %wd_hbm.1, s32[8,128]{1,0:T(8,128)} %bitcast.3, s32[8,128]{1,0:T(8,128)} %bitcast.4, f32[8,128]{1,0:T(8,128)} %bitcast.5), custom_call_target="tpu_custom_call" | custom-call | tf_op jit(solution)/shard_map/pallas_call | solution.py:343
  50.3 0.8 %copy.9 = bf16[128,2048]{1,0:T(8,128)(2,1)} copy(bf16[128,2048]{1,0:T(8,128)(2,1)S(1)} %shard_map.73) | data formatting | bytes 1048576

commit v6 on v5

--- a/solution.py
+++ b/solution.py
@@ -8,12 +8,12 @@
 MESH_ID = pl.DeviceIdType.MESH
 CORES = 2
 BLOCKS = ((0, 0, 512), (1, 1024, 512), (0, 512, 512), (1, 1536, 512))
-LATE = ((1, 0), (1, 1), (2, 2), (3, 3))
+LATE = ((0, 0), (0, 1), (0, 2), (0, 3))
 HALVES = 2
 DOWN_PARTS = 2
 K_SIZES = (512, 512, 512, 512)
 K_PARTS = len(K_SIZES)
-FIRST_ORDER = (0, 1, 2, 3)
+FIRST_ORDER = (1, 0, 3, 2)
 WEIGHT_SLOTS = 3
 VMEM_LIMIT = 62 * 2 ** 20
 BF16_MAX = 3.3895313892515355e38
@@ -234,7 +234,7 @@
             def _():
                 for copy in weight_copies(e + 2):
                     copy.start()
-            for part in range(DOWN_PARTS):
+            for part in reversed(range(DOWN_PARTS)):
                 down_step(e, slot, part * down_size, down_size, hidden)
                 for b in range(n_blocks // 2):
                     if (BLOCKS[b][1] + BLOCKS[b][2] - 1) // down_size == part:
@@ -242,12 +242,12 @@
 
             @pl.when(e == experts - 1)
             def _():
-                for b in range(n_blocks // 2, n_blocks):
+                for b in FIRST_ORDER[n_blocks // 2:]:
                     first_send(b, e - 1)
 
             @pl.when(e != experts - 2)
             def _():
-                for b in range(n_blocks // 2, n_blocks):
+                for b in FIRST_ORDER[n_blocks // 2:]:
                     first_send(b, e)
             keep_own(e)
 
@@ -295,13 +295,16 @@
             def _():
                 for way in range(2):
                     own_copy(b, way).start()
+            if b < n_blocks - 1:
+                acc[:, columns(b)] = partial(b, 0)
         for b in range(n_blocks):
             for way in range(2):
                 far_copy(b, way).wait_recv()
                 part, cols = relay_part(way), columns(b)
                 near_out[way, part, cols] = near_out[way, part, cols] + far_in[way, :, cols]
                 sum_copy(b, way).start()
-            acc[:, columns(b)] = partial(b, 0)
+            if b == n_blocks - 1:
+                acc[:, columns(b)] = partial(b, 0)
         for b in range(n_blocks):
             both_ways(b, sum_here).wait_recv()
             late = [n for trigger, n in LATE if trigger == b]

time: 51.1 us -> 50.9 us (level)
  no operation moved by 1% of the time
where the time goes in v6:
time: 50.9 us; the launch traced here: 50.8 us
  Pallas kernels  50 us (98%)
  local copies, waits for them, and re-layouts  0.8 us (2%)
    pallas_call x1, Pallas kernels, local_step(): pl.pallas_call(make_kernel(ring, experts, capacity, width, ff, tokens, to...  50 us

profile of v6, /device:TPU:96, one launch (start us, length us, event | category | flops | bytes accessed | tf_op | source)
XLA Modules:
  0.0 50.8 jit_solution(4904231857145111159)
XLA Ops:
  0.0 50.0 %shard_map.73 = bf16[128,2048]{1,0:T(8,128)(2,1)S(1)} custom-call(bf16[32,4,8,2048]{3,2,1,0:T(8,128)(2,1)} %x_hbm.1, bf16[4,2048,768]{2,1,0:T(8,128)(2,1)} %wg_hbm.1, bf16[4,2048,768]{2,1,0:T(8,128)(2,1)} %wu_hbm.1, bf16[4,768,2048]{2,1,0:T(8,128)(2,1)} %wd_hbm.1, s32[8,128]{1,0:T(8,128)} %bitcast.3, s32[8,128]{1,0:T(8,128)} %bitcast.4, f32[8,128]{1,0:T(8,128)} %bitcast.5), custom_call_target="tpu_custom_call" | custom-call | tf_op jit(solution)/shard_map/pallas_call | solution.py:346
  50.0 0.8 %copy.9 = bf16[128,2048]{1,0:T(8,128)(2,1)} copy(bf16[128,2048]{1,0:T(8,128)(2,1)S(1)} %shard_map.73) | data formatting | bytes 1048576

commit v7 on v6

--- a/solution.py
+++ b/solution.py
@@ -131,13 +131,13 @@
 
         def part_copies(k):
             cols = k_slice(k)
-            return (pltpu.make_async_copy(x_hbm.at[:, 0, :, cols], x_buf.at[0, :, :, cols], part_sem.at[0, k]),
-                    pltpu.make_async_copy(wg_hbm.at[0, cols], wg_buf.at[0, cols], part_sem.at[1, k]),
-                    pltpu.make_async_copy(wu_hbm.at[0, cols], wu_buf.at[0, cols], part_sem.at[2, k]))
+            return (pltpu.make_async_copy(x_hbm.at[:, 0, :, cols], x_buf.at[0, :, :, cols], (weight_sem.at[0, 0] if k == 0 else part_sem.at[0, k - 1])),
+                    pltpu.make_async_copy(wg_hbm.at[0, cols], wg_buf.at[0, cols], (weight_sem.at[1, 0] if k == 0 else part_sem.at[1, k - 1])),
+                    pltpu.make_async_copy(wu_hbm.at[0, cols], wu_buf.at[0, cols], (weight_sem.at[2, 0] if k == 0 else part_sem.at[2, k - 1])))
 
         def down_part_copy(b):
             cols = columns(b)
-            return pltpu.make_async_copy(wd_hbm.at[0, :, cols], wd_buf.at[0, :, cols], down_sem.at[b])
+            return pltpu.make_async_copy(wd_hbm.at[0, :, cols], wd_buf.at[0, :, cols], (weight_sem.at[3, 0] if b == FIRST_ORDER[0] else down_sem.at[b - int(b > FIRST_ORDER[0])]))
 
         def weight_copies(e):
             slot = lax.rem(e, WEIGHT_SLOTS)
@@ -366,8 +366,8 @@
                 pltpu.VMEM((2, tokens, width), f32),
                 pltpu.VMEM((2, tokens, width), f32),
                 pltpu.VMEM((tokens, width), f32),
-                dma((3, K_PARTS)),
-                dma((n_blocks,)),
+                dma((3, K_PARTS - 1)),
+                dma((n_blocks - 1,)),
                 dma((4, 2)),
                 dma((3,)),
                 dma((1,)),

time: 50.9 us -> 50.9 us (level)
  no operation moved by 1% of the time
where the time goes in v7:
time: 50.9 us; the launch traced here: 50.8 us
  Pallas kernels  50 us (98%)
  local copies, waits for them, and re-layouts  0.8 us (2%)
    pallas_call x1, Pallas kernels, local_step(): pl.pallas_call(make_kernel(ring, experts, capacity, width, ff, tokens, to...  50 us

profile of v7, /device:TPU:96, one launch (start us, length us, event | category | flops | bytes accessed | tf_op | source)
XLA Modules:
  0.0 50.8 jit_solution(12930508016760978819)
XLA Ops:
  0.0 50.0 %shard_map.73 = bf16[128,2048]{1,0:T(8,128)(2,1)S(1)} custom-call(bf16[32,4,8,2048]{3,2,1,0:T(8,128)(2,1)} %x_hbm.1, bf16[4,2048,768]{2,1,0:T(8,128)(2,1)} %wg_hbm.1, bf16[4,2048,768]{2,1,0:T(8,128)(2,1)} %wu_hbm.1, bf16[4,768,2048]{2,1,0:T(8,128)(2,1)} %wd_hbm.1, s32[8,128]{1,0:T(8,128)} %bitcast.3, s32[8,128]{1,0:T(8,128)} %bitcast.4, f32[8,128]{1,0:T(8,128)} %bitcast.5), custom_call_target="tpu_custom_call" | custom-call | tf_op jit(solution)/shard_map/pallas_call | solution.py:346
  50.0 0.8 %copy.9 = bf16[128,2048]{1,0:T(8,128)(2,1)} copy(bf16[128,2048]{1,0:T(8,128)(2,1)S(1)} %shard_map.73) | data formatting | bytes 1048576
